TPU v7x, 32 devices: a whole 2x2x4 slice. The times are simulated.
32 devices in a mesh: groups: 2 (over y), expert: 4 (over z), tensor: 2 (over x), sub: 2 (over core).
Axes of the slice: x: 2, y: 2, z: 4, core: 2. Of those that a mesh axis runs over, the one named last changes fastest.
Arguments:
- tokens: bfloat16 [48, 7168], P(('groups', 'expert', 'tensor'), 'sub'), parts along dimension 0, may hold values from -6 to 6
- expert_ids: int32 [48, 8], P(('groups', 'expert', 'tensor')), parts along dimension 0, may hold values from 0 to 15, all different within a row; in each aligned block of 3 rows (0 to 2, 3 to 5, ...) at most 2 rows name the same one
- gate_weights: float32 [48, 8], P(('groups', 'expert', 'tensor')), parts along dimension 0, may hold values from 0.1 to 0.6
- gate_proj: bfloat16 [16, 1024, 7168], P('expert', 'tensor', 'sub'), may hold values from -0.0625 to 0.0625
- up_proj: bfloat16 [16, 1024, 7168], P('expert', 'tensor', 'sub'), may hold values from -0.0625 to 0.0625
- down_proj: bfloat16 [16, 1024, 7168], P('expert', 'tensor', 'sub'), may hold values from -0.1875 to 0.1875
Outputs:
- blended: bfloat16 [48, 7168], P(('groups', 'expert', 'tensor'), 'sub'), parts along dimension 0
There are 2 independent parts, one for each index of `groups`. A program takes and returns all parts, laid end to end along the dimension named above; an argument that names none is the same for every part. Nothing has to cross between parts.
Inputs may be any that keep to these rules, and one draw needn't show every extreme that they name: `expert_ids`: each row names 8 different experts. Among the rows of one owner (aligned blocks of 3 rows) no expert is named by more than 2 rows, a bound that some block reaches.
All inputs are finite; a program needn't handle non-finite values.
Results may differ from a plain program's by a relative error of at most 0.02.
Values may be sent and summed in bfloat16 or wider, within the bound.
A program may use at most 128 MiB of HBM per device.

v0:
```python
import jax
import jax.numpy as jnp
from jax import lax
from jax.sharding import PartitionSpec as P

SLOTS = 2


def per_device(tokens, expert_ids, gate_weights, gate_proj, up_proj, down_proj):
    expert_count = lax.axis_size("expert")
    tensor_count = lax.axis_size("tensor")
    local_count = gate_proj.shape[0]
    total_experts = expert_count * local_count
    features = tokens.shape[1]
    owned = tokens.shape[0]
    labels = jnp.arange(total_experts, dtype=jnp.int32)
    chosen = expert_ids[:, :, None] == labels[None, None, :]
    picked = jnp.sum(chosen.astype(jnp.int32), axis=1)
    before = jnp.cumsum(picked, axis=0) - picked
    slot_ids = jnp.arange(SLOTS, dtype=jnp.int32)
    placed = (picked[:, :, None] == 1) & (before[:, :, None] == slot_ids[None, None, :])
    placed_flat = placed.reshape(owned, total_experts * SLOTS)
    outgoing = jnp.dot(
        placed_flat.astype(jnp.bfloat16).T, tokens, preferred_element_type=jnp.float32
    ).astype(jnp.bfloat16)
    slab = local_count * SLOTS * features
    outgoing = outgoing.reshape(expert_count, slab)
    peers = expert_count * tensor_count
    copies = jnp.broadcast_to(outgoing[:, None, :], (expert_count, tensor_count, slab)).reshape(
        peers, slab
    )
    arrived = lax.all_to_all(copies, ("expert", "tensor"), split_axis=0, concat_axis=0, tiled=True)
    rows_in = jnp.moveaxis(arrived.reshape(peers, local_count, SLOTS, features), 1, 0)
    rows_in = rows_in.reshape(local_count, peers * SLOTS, features)
    gate_part = jnp.einsum("lrd,lfd->lrf", rows_in, gate_proj, preferred_element_type=jnp.float32)
    up_part = jnp.einsum("lrd,lfd->lrf", rows_in, up_proj, preferred_element_type=jnp.float32)
    gate_full, up_full = (
        lax.psum(gate_part.astype(jnp.bfloat16), "sub").astype(jnp.float32),
        lax.psum(up_part.astype(jnp.bfloat16), "sub").astype(jnp.float32),
    )
    hidden = (jax.nn.silu(gate_full) * up_full).astype(jnp.bfloat16)
    partial_value = jnp.einsum(
        "lrf,lfd->lrd", hidden, down_proj, preferred_element_type=jnp.float32
    ).astype(jnp.bfloat16)
    partial_value = jnp.moveaxis(
        partial_value.reshape(local_count, peers, SLOTS, features), 0, 1
    ).reshape(peers, slab)
    returned = lax.all_to_all(
        partial_value, ("expert", "tensor"), split_axis=0, concat_axis=0, tiled=True
    )
    returned = returned.reshape(expert_count, tensor_count, slab)
    results = jnp.sum(returned.astype(jnp.float32), axis=1).reshape(total_experts * SLOTS, features)
    weight_table = jnp.sum(gate_weights[:, :, None] * chosen.astype(jnp.float32), axis=1)
    mixing = (weight_table[:, :, None] * placed.astype(jnp.float32)).reshape(
        owned, total_experts * SLOTS
    )
    blended = jnp.dot(mixing, results, precision=lax.Precision.HIGHEST)
    return blended.astype(jnp.bfloat16)


def solution(mesh):
    placed = (
        P(("groups", "expert", "tensor"), "sub"),
        P(("groups", "expert", "tensor"), None),
        P(("groups", "expert", "tensor"), None),
        P("expert", "tensor", "sub"),
        P("expert", "tensor", "sub"),
        P("expert", "tensor", "sub"),
    )
    return jax.shard_map(
        per_device,
        mesh=mesh,
        in_specs=placed,
        out_specs=P(("groups", "expert", "tensor"), "sub"),
        check_vma=False,
    )
```

profile of v0, /device:TPU:0, one launch (start us, length us, event | category | flops | bytes accessed | tf_op | source)
XLA Modules:
  0.0 119.9 jit_solution(9019192052215831962)
XLA Ops:
  6.5 0.0 copy-start
  6.5 0.0 all-reduce.3.cloned.1.call-start
  6.5 0.8 convert_reduce_fusion.1
  7.4 0.1 and.21
  7.4 0.1 and.23
  7.6 0.1 eq.66
  7.6 0.1 eq.61
  7.7 0.1 eq.64
  7.8 0.0 copy-done
  7.8 0.3 convolution_convert_fusion.1
  8.1 0.2 broadcast_in_dim.4
  8.3 0.2 broadcast_in_dim.5
  8.5 0.5 all_to_all.16
  9.0 0.5 broadcast.69
  9.5 3.5 %reduce.3 = bf16[8,28672]{1,0:T(8,128)(2,1)S(1)} reduce(bf16[8,1,28672]{2,1,0:T(2,128)(2,1)S(1)} %all_to_all.16, bf16[]{:T(256)} %broadcast.69), dimensions={1}, to_apply=%all_to_all.16.reduce_sub_computation | reduce | bytes 917506 | tf_op jit(solution)/shard_map/all_to_all | solution.py:32
  13.0 0.3 reshape.94
  13.4 20.3 %all_to_all.20 = bf16[8,2,14336]{2,1,0:T(2,128)(2,1)S(1)} all-to-all(bf16[8,2,14336]{2,1,0:T(2,128)(2,1)S(1)} %reshape.94), channel_id=1, replica_groups=mesh['groups'=2,'expert'=4,'tensor'=2,'sub'=2] {'expert','tensor'}, dimensions={0} | all-to-all | bytes 917504 | tf_op jit(solution)/shard_map/all_to_all | solution.py:32
  33.7 0.5 reshape.95
  34.1 2.9 %reduce = bf16[8,28672]{1,0:T(8,128)(2,1)S(1)} reduce(bf16[8,1,28672]{2,1,0:T(2,128)(2,1)S(1)} %reshape.95, bf16[]{:T(256)} %constant.17), dimensions={1}, to_apply=%all_to_all.13.reduce_sub_computation | reduce | bytes 917506 | tf_op jit(solution)/shard_map/all_to_all | solution.py:32
  37.0 0.3 reshape.87
  37.3 0.3 copy.17
  37.7 0.2 reshape.88
  37.9 9.7 %convolution_convert_fusion.3 = bf16[4,16,512]{2,1,0:T(8,128)(2,1)} fusion(bf16[4,16,3584]{2,1,0:T(8,128)(2,1)S(1)} %reshape.88, bf16[4,512,3584]{2,1,0:T(8,128)(2,1)} %param.10), kind=kOutput, calls=%fused_computation.3 | convolution fusion | flops 234913792 | bytes 15204352 | tf_op jit(solution)/shard_map/lrd,lfd->lrf/dot_general | solution.py:36
  47.5 9.7 %convolution_convert_fusion.4 = bf16[4,16,512]{2,1,0:T(8,128)(2,1)} fusion(bf16[4,16,3584]{2,1,0:T(8,128)(2,1)S(1)} %reshape.88, bf16[4,512,3584]{2,1,0:T(8,128)(2,1)} %param.9), kind=kOutput, calls=%fused_computation.4 | convolution fusion | flops 234913792 | bytes 15204352 | tf_op jit(solution)/shard_map/lrd,lfd->lrf/dot_general | solution.py:35
  57.2 0.0 copy-start.1
  57.2 0.0 copy-start.2
  57.2 0.0 all-reduce.3.cloned.1.call-update
  57.3 17.1 %all-reduce.3.cloned.1.call-done = (bf16[4,16,512]{2,1,0:T(8,128)(2,1)}, bf16[4,16,512]{2,1,0:T(8,128)(2,1)}) async-done(((bf16[4,16,512]{2,1,0:T(8,128)(2,1)}, bf16[4,16,512]{2,1,0:T(8,128)(2,1)}), (bf16[4,16,512]{2,1,0:T(8,128)(2,1)}, bf16[4,16,512]{2,1,0:T(8,128)(2,1)})) %all-reduce.3.cloned.1.call-update) | async-done | bytes 131088 | tf_op jit(solution)/shard_map/psum | solution.py:39
  74.4 7.3 %convolution_convert_fusion = bf16[4,16,3584]{2,1,0:T(8,128)(2,1)S(1)} fusion(bf16[4,512,3584]{2,1,0:T(8,128)(2,1)} %param.11, bf16[4,16,512]{2,1,0:T(8,128)(2,1)} %get-tuple-element.5, bf16[4,16,512]{2,1,0:T(8,128)(2,1)} %get-tuple-element.6), kind=kOutput, calls=%fused_computation | convolution fusion | flops 235372544 | bytes 15269888 | tf_op jit(solution)/shard_map/lrf,lfd->lrd/dot_general | solution.py:42
  81.6 0.2 reshape.89
  81.8 0.3 copy.22
  82.1 0.6 all_to_all.17
  82.8 3.5 %reduce.4 = bf16[8,28672]{1,0:T(8,128)(2,1)S(1)} reduce(bf16[8,1,28672]{2,1,0:T(2,128)(2,1)S(1)} %all_to_all.17, bf16[]{:T(256)} %broadcast.69), dimensions={1}, to_apply=%all_to_all.17.reduce_sub_computation | reduce | bytes 917506 | tf_op jit(solution)/shard_map/all_to_all | solution.py:48
  86.3 1.1 reshape.96
  87.4 5.8 %all-to-all-start.1 = ((bf16[8,2,14336]{2,1,0:T(2,128)(2,1)}), bf16[8,2,14336]{2,1,0:T(2,128)(2,1)S(1)}, u32[]{:S(2)}, u32[]{:S(2)}) async-start(bf16[8,2,14336]{2,1,0:T(2,128)(2,1)} %reshape.96), calls=%async_computation.1 | async-start | bytes 917504 | tf_op jit(solution)/shard_map/all_to_all | solution.py:48
  93.2 0.0 copy-done.1
  93.2 0.0 copy-done.2
  93.2 0.1 select_reduce_fusion
  93.3 0.1 fusion.8
  93.4 0.1 mul.29
  93.5 13.2 %all-to-all-done.1 = bf16[8,2,14336]{2,1,0:T(2,128)(2,1)S(1)} async-done(((bf16[8,2,14336]{2,1,0:T(2,128)(2,1)}), bf16[8,2,14336]{2,1,0:T(2,128)(2,1)S(1)}, u32[]{:S(2)}, u32[]{:S(2)}) %all-to-all-start.1) | async-done | bytes 458784 | tf_op jit(solution)/shard_map/all_to_all | solution.py:48
  106.7 0.5 reshape.97
  107.2 2.7 %convert_reduce_fusion = f32[8,28672]{1,0:T(8,128)S(1)} fusion(bf16[8,1,28672]{2,1,0:T(2,128)(2,1)S(1)} %reshape.97), kind=kLoop, calls=%fused_computation.5 | loop fusion | flops 229376 | bytes 1376256 | tf_op jit(solution)/shard_map/convert_element_type | solution.py:52
  109.9 0.5 reshape.91
  110.4 1.3 %reduce_sum.29 = f32[4,28672]{1,0:T(4,128)S(1)} reduce(f32[4,2,28672]{2,1,0:T(2,128)S(1)} %reshape.91, f32[]{:T(128)} %constant.12.clone.1), dimensions={1}, to_apply=%region_5.6 | reduce | flops 114688 | bytes 1376260 | tf_op jit(solution)/shard_map/reduce_sum | solution.py:52
  111.7 0.3 reshape.90
  112.1 0.9 convolution_convert_fusion.2
  (4 shorter events, 0.1 us)
Async XLA Ops:
  6.5 1.3 %copy-start = (bf16[3,3584]{1,0:T(4,128)(2,1)S(1)}, bf16[3,3584]{1,0:T(4,128)(2,1)}, u32[]{:S(2)}) copy-start(bf16[3,3584]{1,0:T(4,128)(2,1)} %param.6) | copy-start | bytes 64516
  6.5 67.8 %all-reduce.3.cloned.1.call-start = ((), (), s32[]{:S(2)}) async-start(), calls=%async_computation.2 | async-start | bytes 262144 | tf_op jit(solution)/shard_map/psum | solution.py:39
  57.2 36.0 %copy-start.1 = (s32[3,8]{1,0:T(4,128)S(1)}, s32[3,8]{1,0:T(4,128)}, u32[]{:S(2)}) copy-start(s32[3,8]{1,0:T(4,128)} %param.7) | copy-start | bytes 292
  57.2 36.0 %copy-start.2 = (f32[3,8]{1,0:T(4,128)S(1)}, f32[3,8]{1,0:T(4,128)}, u32[]{:S(2)}) copy-start(f32[3,8]{1,0:T(4,128)} %param.8) | copy-start | bytes 292
  87.4 19.3 %all-to-all-start.1 = ((bf16[8,2,14336]{2,1,0:T(2,128)(2,1)}), bf16[8,2,14336]{2,1,0:T(2,128)(2,1)S(1)}, u32[]{:S(2)}, u32[]{:S(2)}) async-start(bf16[8,2,14336]{2,1,0:T(2,128)(2,1)} %reshape.96), calls=%async_computation.1 | async-start | bytes 917504 | tf_op jit(solution)/shard_map/all_to_all | solution.py:48
Sparse Core Ops, SparseCore 0:
  57.4 16.9 all-reduce.2
where the time goes:
time: 120 us
  waiting for transfers between devices  30.3 us (25%)
  matrix products  27.8 us (23%)
  blocking collectives  20.3 us (17%)
  other arithmetic  15 us (12%)
  between operations  13.6 us (11%)
  local copies, waits for them, and re-layouts  7.07 us (6%)
  starting transfers between devices  5.82 us (5%)
    all_to_all x1, blocking collectives, per_device(): lax.all_to_all(copies, ('expert', 'tensor'), split_axis=0, concat_axis=0,...  20.3 us
    psum x1, waiting for transfers between devices, per_device(): lax.psum(up_part.astype(jnp.bfloat16), 'sub').astype(jnp.float32)  17.1 us
    all_to_all x1, waiting for transfers between devices, per_device(): lax.all_to_all(partial_value, ('expert', 'tensor'), split_axis=0, concat_...  13.2 us
    dot_general x1, matrix products, per_device(): jnp.einsum('lrd,lfd->lrf', rows_in, up_proj, preferred_element_type=jnp.f...  9.69 us
    dot_general x1, matrix products, per_device(): jnp.einsum('lrd,lfd->lrf', rows_in, gate_proj, preferred_element_type=jnp...  9.68 us
    dot_general x1, matrix products, per_device(): jnp.einsum('lrf,lfd->lrd', hidden, down_proj, preferred_element_type=jnp....  7.26 us
    all_to_all x2, other arithmetic, per_device(): lax.all_to_all(copies, ('expert', 'tensor'), split_axis=0, concat_axis=0,...  6.41 us
    all_to_all x1, starting transfers between devices, per_device(): lax.all_to_all(partial_value, ('expert', 'tensor'), split_axis=0, concat_...  5.81 us
  transfers between devices with their start and end apart: 2, of which 2 were waited for; matrix products, arithmetic and copies ran while one was open for 0% of the time, Pallas kernels for 0%

commit v1 on v0

v1 whole, which is shorter than its diff:
```python
import functools

import jax
import jax.numpy as jnp
from jax import lax
from jax.experimental import pallas as pl
from jax.experimental.pallas import tpu as pltpu
from jax.sharding import PartitionSpec as P

MESH = pl.DeviceIdType.MESH
PIECES = 2
EARLY = 2
NT = (((1,), (1,)), ((), ()))


def kernel(
    sizes,
    tok_ref, ids_ref, gw_ref, gate_ref, up_ref, down_ref, out_ref,
    wg, wu, wd, tok_in, ids_in, gw_in, x32, x16, ids_all, gw_all,
    own_part, sent_part, got_part, hidden, y, stage, ret,
    w_sem, in_send, in_recv, part_send, part_recv, ret_send, ret_recv,
):
    expert_count, tensor_count, sub_count = sizes
    peers = expert_count * tensor_count
    local_count, units = gate_ref.shape[0], gate_ref.shape[1]
    owned, features = tok_ref.shape
    width = features // PIECES
    expert_at = lax.axis_index("expert")
    me = expert_at * tensor_count + lax.axis_index("tensor")
    sub = lax.axis_index("sub")

    def peer(k):
        p = lax.rem(me + k, peers)
        return p, {"expert": p // tensor_count, "tensor": lax.rem(p, tensor_count)}

    def core(j):
        return {"sub": lax.rem(sub + j, sub_count)}

    barrier = pltpu.get_barrier_semaphore()

    def greet(k, carry):
        pl.semaphore_signal(barrier, inc=1, device_id=peer(k)[1], device_id_type=MESH)
        return carry

    lax.fori_loop(1, peers, greet, 0)
    for j in range(1, sub_count):
        pl.semaphore_signal(barrier, inc=1, device_id=core(j), device_id_type=MESH)

    loads = []
    for l in range(local_count):
        loads.append(pltpu.make_async_copy(gate_ref.at[l], wg.at[l], w_sem.at[0, l]))
        loads.append(pltpu.make_async_copy(up_ref.at[l], wu.at[l], w_sem.at[1, l]))
    for l in range(local_count):
        loads.append(pltpu.make_async_copy(down_ref.at[l], wd.at[l], w_sem.at[2, l]))
    inputs = ((tok_ref, tok_in), (ids_ref, ids_in), (gw_ref, gw_in))
    for i, (src, dst) in enumerate(inputs):
        pltpu.make_async_copy(src, dst.at[me], in_recv.at[i]).start()
    early = 2 * min(EARLY, local_count)
    for load in loads[:early]:
        load.start()

    pl.semaphore_wait(barrier, peers - 1 + sub_count - 1)

    def dispatch(k, carry):
        _, where = peer(k)
        for i, (src, dst) in enumerate(inputs):
            pltpu.make_async_remote_copy(
                src_ref=src, dst_ref=dst.at[me], send_sem=in_send.at[i], recv_sem=in_recv.at[i],
                device_id=where, device_id_type=MESH,
            ).start()
        return carry

    lax.fori_loop(1, peers, dispatch, 0)
    for load in loads[early:]:
        load.start()

    for i, (_, dst) in enumerate(inputs):
        pltpu.make_async_copy(dst, dst, in_recv.at[i]).wait()
    for p in range(peers):
        rows = pl.ds(p * owned, owned)
        x32[rows, :] = tok_in[p].astype(jnp.float32)
        ids_all[rows, :] = ids_in[p]
        gw_all[rows, :] = gw_in[p]
    x16[...] = x32[...].astype(jnp.bfloat16)

    def first(l):
        x = x16[...]
        loads[2 * l].wait()
        gate = lax.dot_general(x, wg[l], NT, preferred_element_type=jnp.float32)
        own_part[l, :, :units] = gate
        sent_part[l, :, :units] = gate.astype(jnp.bfloat16)
        loads[2 * l + 1].wait()
        up = lax.dot_general(x, wu[l], NT, preferred_element_type=jnp.float32)
        own_part[l, :, units:] = up
        sent_part[l, :, units:] = up.astype(jnp.bfloat16)
        for j in range(1, sub_count):
            exchange(l, j).start()

    def exchange(l, j):
        return pltpu.make_async_remote_copy(
            src_ref=sent_part.at[l], dst_ref=got_part.at[l, j - 1],
            send_sem=part_send.at[l, j - 1], recv_sem=part_recv.at[l, j - 1],
            device_id=core(j), device_id_type=MESH,
        )

    def finish(l):
        both = own_part[l]
        for j in range(1, sub_count):
            exchange(l, j).wait()
            both = both + got_part[l, j - 1].astype(jnp.float32)
        gate, up = both[:, :units], both[:, units:]
        label = expert_at * local_count + l
        weight = jnp.sum(jnp.where(ids_all[...] == label, gw_all[...], 0.0), axis=1, keepdims=True)
        hidden[l] = (gate / (1.0 + jnp.exp(-gate)) * up * weight).astype(jnp.bfloat16)

    for l in range(local_count):
        first(l)
        if l > 0:
            finish(l - 1)
    last = local_count - 1
    for l in range(last):
        loads[2 * local_count + l].wait()
        part = jnp.dot(hidden[l], wd[l], preferred_element_type=jnp.float32)
        y[...] = part if l == 0 else y[...] + part
    finish(last)
    loads[2 * local_count + last].wait()

    for c in range(PIECES):
        columns = pl.ds(c * width, width)
        part = jnp.dot(hidden[last], wd[last, :, columns], preferred_element_type=jnp.float32)
        if last > 0:
            part = part + y[:, columns]
        for p in range(peers):
            stage[c, p] = part[p * owned:(p + 1) * owned].astype(jnp.bfloat16)

        def give(k, carry):
            p, where = peer(k)
            pltpu.make_async_remote_copy(
                src_ref=stage.at[c, p], dst_ref=ret.at[c, me], send_sem=ret_send.at[c],
                recv_sem=ret_recv.at[c], device_id=where, device_id_type=MESH,
            ).start()
            return carry

        lax.fori_loop(1, peers, give, 0)

    for c in range(PIECES):
        columns = pl.ds(c * width, width)
        some = ret.at[c, pl.ds(0, peers - 1)]
        pltpu.make_async_copy(some, some, ret_recv.at[c]).wait()
        total = stage[c, me].astype(jnp.float32)
        for k in range(1, peers):
            total = total + ret[c, peer(k)[0]].astype(jnp.float32)
        out_ref[:, columns] = total.astype(jnp.bfloat16)

    for i, (_, dst) in enumerate(inputs):
        some = dst.at[pl.ds(0, peers - 1)]
        pltpu.make_async_copy(some, some, in_send.at[i]).wait()
    for c in range(PIECES):
        some = ret.at[c, pl.ds(0, peers - 1)]
        pltpu.make_async_copy(some, some, ret_send.at[c]).wait()


def solution(mesh):
    expert_count, tensor_count = mesh.shape["expert"], mesh.shape["tensor"]
    sub_count = mesh.shape["sub"]
    peers = expert_count * tensor_count

    def per_device(tokens, expert_ids, gate_weights, gate_proj, up_proj, down_proj):
        owned, features = tokens.shape
        top = expert_ids.shape[1]
        local_count, units = gate_proj.shape[0], gate_proj.shape[1]
        rows = peers * owned
        others = max(1, sub_count - 1)
        width = features // PIECES
        bf16, f32 = jnp.bfloat16, jnp.float32
        dma = pltpu.SemaphoreType.DMA
        hbm = pl.BlockSpec(memory_space=pl.ANY)
        return pl.pallas_call(
            functools.partial(kernel, (expert_count, tensor_count, sub_count)),
            out_shape=jax.ShapeDtypeStruct((owned, features), bf16),
            in_specs=[hbm] * 6,
            out_specs=pl.BlockSpec(memory_space=pltpu.VMEM),
            scratch_shapes=[
                pltpu.VMEM(gate_proj.shape, bf16),
                pltpu.VMEM(up_proj.shape, bf16),
                pltpu.VMEM(down_proj.shape, bf16),
                pltpu.VMEM((peers, owned, features), bf16),
                pltpu.VMEM((peers, owned, top), jnp.int32),
                pltpu.VMEM((peers, owned, top), f32),
                pltpu.VMEM((rows, features), f32),
                pltpu.VMEM((rows, features), bf16),
                pltpu.VMEM((rows, top), jnp.int32),
                pltpu.VMEM((rows, top), f32),
                pltpu.VMEM((local_count, rows, 2 * units), f32),
                pltpu.VMEM((local_count, rows, 2 * units), bf16),
                pltpu.VMEM((local_count, others, rows, 2 * units), bf16),
                pltpu.VMEM((local_count, rows, units), bf16),
                pltpu.VMEM((rows, features), f32),
                pltpu.VMEM((PIECES, peers, owned, width), bf16),
                pltpu.VMEM((PIECES, peers, owned, width), bf16),
                dma((3, local_count)),
                dma((3,)),
                dma((3,)),
                dma((local_count, others)),
                dma((local_count, others)),
                dma((PIECES,)),
                dma((PIECES,)),
            ],
            compiler_params=pltpu.CompilerParams(
                collective_id=0, has_side_effects=True, vmem_limit_bytes=60 * 1024 * 1024
            ),
        )(tokens, expert_ids, gate_weights, gate_proj, up_proj, down_proj)

    placed = (
        P(("groups", "expert", "tensor"), "sub"),
        P(("groups", "expert", "tensor"), None),
        P(("groups", "expert", "tensor"), None),
        P("expert", "tensor", "sub"),
        P("expert", "tensor", "sub"),
        P("expert", "tensor", "sub"),
    )
    return jax.shard_map(
        per_device,
        mesh=mesh,
        in_specs=placed,
        out_specs=P(("groups", "expert", "tensor"), "sub"),
        check_vma=False,
    )
```

time: 120 us -> 33.6 us (0.28)
  Pallas kernels: 0 us -> 32 us
  waiting for transfers between devices: 30.3 us -> 0 us
  matrix products: 27.8 us -> 0 us
  blocking collectives: 20.3 us -> 0 us
  other arithmetic: 15 us -> 0 us
  between operations: 13.6 us -> 0.01 us
  starting transfers between devices: 5.82 us -> 0 us
  local copies, waits for them, and re-layouts: 7.07 us -> 1.37 us
    pallas_call x0 -> x1, Pallas kernels: none -> 32 us  [per_device(): pl.pallas_call(functools.partial(kernel, (expert_count, tensor_count, sub...]
    dot_general x5 -> x0, matrix products: 27.8 us -> none  [the longest x1 9.69 us: per_device(): jnp.einsum('lrd,lfd->lrf', rows_in, up_proj, preferred_element_type=jnp.f...]
    all_to_all x1 -> x0, blocking collectives: 20.3 us -> none  [per_device(): lax.all_to_all(copies, ('expert', 'tensor'), split_axis=0, concat_axis=0,...]
    psum x1 -> x0, waiting for transfers between devices: 17.1 us -> none  [per_device(): lax.psum(up_part.astype(jnp.bfloat16), 'sub').astype(jnp.float32)]
    all_to_all x1 -> x0, waiting for transfers between devices: 13.2 us -> none  [per_device(): lax.all_to_all(partial_value, ('expert', 'tensor'), split_axis=0, concat_...]
    all_to_all x3 -> x0, other arithmetic: 9.94 us -> none  [the longest x2 6.41 us: per_device(): lax.all_to_all(copies, ('expert', 'tensor'), split_axis=0, concat_axis=0,...]
    all_to_all x1 -> x0, starting transfers between devices: 5.81 us -> none  [per_device(): lax.all_to_all(partial_value, ('expert', 'tensor'), split_axis=0, concat_...]
    convert_element_type x1 -> x0, other arithmetic: 2.68 us -> none  [per_device(): returned.astype(jnp.float32)]
  transfers between devices with their start and end apart: 2 -> 0, of which waited for: 2 -> 0; matrix products, arithmetic and copies ran while one was open for 0% -> 0% of each run, Pallas kernels for 0% -> 0%
where the time goes in v1:
time: 33.6 us; the launch traced here: 33.4 us
  Pallas kernels  32 us (95%)
  local copies, waits for them, and re-layouts  1.37 us (4%)
    pallas_call x1, Pallas kernels, per_device(): pl.pallas_call(functools.partial(kernel, (expert_count, tensor_count, sub...  32 us
    unnamed x1, local copies, waits for them, and re-layouts  1.37 us

profile of v1, /device:TPU:0, one launch (start us, length us, event | category | flops | bytes accessed | tf_op | source)
XLA Modules:
  0.0 33.4 jit_solution(1589117850877252329)
XLA Ops:
  0.0 32.0 %shard_map.64 = bf16[3,3584]{1,0:T(4,128)(2,1)} custom-call(bf16[3,3584]{1,0:T(4,128)(2,1)} %tok_ref.1, s32[3,8]{1,0:T(4,128)} %ids_ref.1, f32[3,8]{1,0:T(4,128)} %gw_ref.1, bf16[4,512,3584]{2,1,0:T(8,128)(2,1)} %gate_ref.1, bf16[4,512,3584]{2,1,0:T(8,128)(2,1)} %up_ref.1, bf16[4,512,3584]{2,1,0:T(8,128)(2,1)} %down_ref.1), custom_call_target="tpu_custom_call" | custom-call | tf_op jit(solution)/shard_map/pallas_call | solution.py:178
  32.0 1.4 %copy.8 = bf16[3,3584]{1,0:T(4,128)(2,1)} copy(bf16[3,3584]{1,0:T(4,128)(2,1)} %shard_map.64) | data formatting | bytes 43008

commit v2 on v1

--- a/solution.py
+++ b/solution.py
@@ -8,7 +8,8 @@
 from jax.sharding import PartitionSpec as P
 
 MESH = pl.DeviceIdType.MESH
-PIECES = 2
+PIECES = 1
+TURNED = 2
 EARLY = 2
 NT = (((1,), (1,)), ((), ()))
 
@@ -18,7 +19,7 @@
     tok_ref, ids_ref, gw_ref, gate_ref, up_ref, down_ref, out_ref,
     wg, wu, wd, tok_in, ids_in, gw_in, x32, x16, ids_all, gw_all,
     own_part, sent_part, got_part, hidden, y, stage, ret,
-    w_sem, in_send, in_recv, part_send, part_recv, ret_send, ret_recv,
+    turned, w_sem, in_send, in_recv, part_send, part_recv, ret_send, ret_recv,
 ):
     expert_count, tensor_count, sub_count = sizes
     peers = expert_count * tensor_count
@@ -42,7 +43,7 @@
         pl.semaphore_signal(barrier, inc=1, device_id=peer(k)[1], device_id_type=MESH)
         return carry
 
-    lax.fori_loop(1, peers, greet, 0)
+    lax.fori_loop(1, peers, greet, 0, unroll=peers <= 16)
     for j in range(1, sub_count):
         pl.semaphore_signal(barrier, inc=1, device_id=core(j), device_id_type=MESH)
 
@@ -70,10 +71,16 @@
             ).start()
         return carry
 
-    lax.fori_loop(1, peers, dispatch, 0)
+    lax.fori_loop(1, peers, dispatch, 0, unroll=peers <= 16)
     for load in loads[early:]:
         load.start()
 
+    stage[...] = jnp.zeros_like(stage)
+    for l in range(min(TURNED, local_count)):
+        loads[2 * l].wait()
+        turned[2 * l] = wg[l].T
+        loads[2 * l + 1].wait()
+        turned[2 * l + 1] = wu[l].T
     for i, (_, dst) in enumerate(inputs):
         pltpu.make_async_copy(dst, dst, in_recv.at[i]).wait()
     for p in range(peers):
@@ -85,6 +92,16 @@
 
     def first(l):
         x = x16[...]
+        if l < TURNED:
+            gate = jnp.dot(x, turned[2 * l], preferred_element_type=jnp.float32)
+            up = jnp.dot(x, turned[2 * l + 1], preferred_element_type=jnp.float32)
+            own_part[l, :, :units] = gate
+            sent_part[l, :, :units] = gate.astype(jnp.bfloat16)
+            own_part[l, :, units:] = up
+            sent_part[l, :, units:] = up.astype(jnp.bfloat16)
+            for j in range(1, sub_count):
+                exchange(l, j).start()
+            return
         loads[2 * l].wait()
         gate = lax.dot_general(x, wg[l], NT, preferred_element_type=jnp.float32)
         own_part[l, :, :units] = gate
@@ -131,7 +148,7 @@
         if last > 0:
             part = part + y[:, columns]
         for p in range(peers):
-            stage[c, p] = part[p * owned:(p + 1) * owned].astype(jnp.bfloat16)
+            stage[c, p, :owned] = part[p * owned:(p + 1) * owned].astype(jnp.bfloat16)
 
         def give(k, carry):
             p, where = peer(k)
@@ -141,15 +158,15 @@
             ).start()
             return carry
 
-        lax.fori_loop(1, peers, give, 0)
+        lax.fori_loop(1, peers, give, 0, unroll=peers <= 16)
 
     for c in range(PIECES):
         columns = pl.ds(c * width, width)
         some = ret.at[c, pl.ds(0, peers - 1)]
         pltpu.make_async_copy(some, some, ret_recv.at[c]).wait()
-        total = stage[c, me].astype(jnp.float32)
+        total = stage[c, me, :owned].astype(jnp.float32)
         for k in range(1, peers):
-            total = total + ret[c, peer(k)[0]].astype(jnp.float32)
+            total = total + ret[c, peer(k)[0], :owned].astype(jnp.float32)
         out_ref[:, columns] = total.astype(jnp.bfloat16)
 
     for i, (_, dst) in enumerate(inputs):
@@ -172,6 +189,7 @@
         rows = peers * owned
         others = max(1, sub_count - 1)
         width = features // PIECES
+        padded = pl.cdiv(owned, 4) * 4
         bf16, f32 = jnp.bfloat16, jnp.float32
         dma = pltpu.SemaphoreType.DMA
         hbm = pl.BlockSpec(memory_space=pl.ANY)
@@ -196,8 +214,9 @@
                 pltpu.VMEM((local_count, others, rows, 2 * units), bf16),
                 pltpu.VMEM((local_count, rows, units), bf16),
                 pltpu.VMEM((rows, features), f32),
-                pltpu.VMEM((PIECES, peers, owned, width), bf16),
-                pltpu.VMEM((PIECES, peers, owned, width), bf16),
+                pltpu.VMEM((PIECES, peers, padded, width), bf16),
+                pltpu.VMEM((PIECES, peers, padded, width), bf16),
+                pltpu.VMEM((2 * min(TURNED, local_count), features, units), bf16),
                 dma((3, local_count)),
                 dma((3,)),
                 dma((3,)),

time: 33.6 us -> 31.1 us (0.926)
  Pallas kernels: 32 us -> 29.6 us
    pallas_call x1, Pallas kernels: 32 us -> 29.6 us  [per_device(): pl.pallas_call(functools.partial(kernel, (expert_count, tensor_count, sub...]
where the time goes in v2:
time: 31.1 us; the launch traced here: 30.9 us
  Pallas kernels  29.6 us (95%)
  local copies, waits for them, and re-layouts  1.37 us (4%)
    pallas_call x1, Pallas kernels, per_device(): pl.pallas_call(functools.partial(kernel, (expert_count, tensor_count, sub...  29.6 us
    unnamed x1, local copies, waits for them, and re-layouts  1.37 us

profile of v2, /device:TPU:0, one launch (start us, length us, event | category | flops | bytes accessed | tf_op | source)
XLA Modules:
  0.0 30.9 jit_solution(8612676005173330518)
XLA Ops:
  0.0 29.6 %shard_map.64 = bf16[3,3584]{1,0:T(4,128)(2,1)} custom-call(bf16[3,3584]{1,0:T(4,128)(2,1)} %tok_ref.1, s32[3,8]{1,0:T(4,128)} %ids_ref.1, f32[3,8]{1,0:T(4,128)} %gw_ref.1, bf16[4,512,3584]{2,1,0:T(8,128)(2,1)} %gate_ref.1, bf16[4,512,3584]{2,1,0:T(8,128)(2,1)} %up_ref.1, bf16[4,512,3584]{2,1,0:T(8,128)(2,1)} %down_ref.1), custom_call_target="tpu_custom_call" | custom-call | tf_op jit(solution)/shard_map/pallas_call | solution.py:196
  29.6 1.4 %copy.8 = bf16[3,3584]{1,0:T(4,128)(2,1)} copy(bf16[3,3584]{1,0:T(4,128)(2,1)} %shard_map.64) | data formatting | bytes 43008
